TPU v7x, 32 devices: a whole 2x2x4 slice. The times are simulated.
32 devices in a mesh: groups: 2 (over y), seq: 4 (over z), tp: 4 (over x, core).
Axes of the slice: x: 2, y: 2, z: 4, core: 2. Of those that a mesh axis runs over, the one named last changes fastest.
Arguments:
- q_prefill: bfloat16 [2048, 4096], P(('groups', 'seq'), 'tp'), parts along dimension 0, may hold values from -8 to 8
- k_prefill: bfloat16 [2048, 1024], P(('groups', 'seq'), 'tp'), parts along dimension 0, may hold values from -8 to 8
- v_prefill: bfloat16 [2048, 1024], P(('groups', 'seq'), 'tp'), parts along dimension 0, may hold values from -6 to 6
- pair_lengths: int32 [16], P('groups'), parts along dimension 0, may hold values from 1 to 640, 1024 in all
- q_decode: bfloat16 [8, 4096], P('groups', 'tp'), parts along dimension 0, may hold values from -8 to 8
- cache_k: bfloat16 [8, 256, 1024], P('groups', 'seq', 'tp'), parts along dimension 0, may hold values from -8 to 8
- cache_v: bfloat16 [8, 256, 1024], P('groups', 'seq', 'tp'), parts along dimension 0, may hold values from -6 to 6
- cache_lengths: int32 [8], P('groups'), parts along dimension 0, may hold values from 32 to 256
- stream: bfloat16 [24, 8192], P('groups', 'seq'), parts along dimension 0, may hold values from -40 to 40
- out_weight: bfloat16 [4096, 8192], P('tp', 'seq'), may hold values from -0.09375 to 0.09375
- norm_gain: bfloat16 [8192], P('seq'), may hold values from 0.099609375 to 1.8984375
- vocab_table: bfloat16 [64128, 8192], P('tp', 'seq'), may hold values from -0.0625 to 0.0625
- verdict_ids: int32 [24, 2], P('groups'), parts along dimension 0, may hold values from 0 to 64127
Outputs:
- attended: bfloat16 [2048, 4096], P(('groups', 'seq'), 'tp'), parts along dimension 0
- verdict_hidden: bfloat16 [24, 8192], P('groups', 'seq'), parts along dimension 0
- win: float32 [24], P('groups'), parts along dimension 0
There are 2 independent parts, one for each index of `groups`. A program takes and returns all parts, laid end to end along the dimension named above; an argument that names none is the same for every part. Nothing has to cross between parts.
Inputs may be any that keep to these rules, and one draw needn't show every extreme that they name: `pair_lengths`: the segments lie end to end from position 0 and each is at most 640 long.
All inputs are finite; a program needn't handle non-finite values.
Results may differ from a plain program's by a relative error of at most 0.008.
Values may be sent and summed in bfloat16 or wider, within the bound.
A program may use at most 128 MiB of HBM per device.

v0:
```python
import jax
import jax.numpy as jnp
from jax import lax
from jax.sharding import PartitionSpec as P

D = 8192
H = 32
KVH = 8
HD = 128
PROMPTS = 4


masked_score = -1e30
norm_eps = 1e-05


def joined(value, axis, join):
    pieces = jax.tree.map(lambda part: lax.all_gather(part, axis), value)
    head = jax.tree.map(lambda part: part[0], pieces)
    tail = jax.tree.map(lambda part: part[1:], pieces)
    so_far, _ = lax.scan(lambda so_far, section: (join(so_far, section), None), head, tail)
    return so_far


def segment_of(positions, pair_ends):
    return jnp.sum((pair_ends[None, :] <= positions[:, None]).astype(jnp.int32), axis=1)


def block_rows(row_count, tokens):
    for factor in (4, 3, 2):
        return tokens * factor
    return row_count


def merge_partials(first, second):
    max_first, total_first, sum_first = first
    max_second, total_second, sum_second = second
    new_max = jnp.maximum(max_first, max_second)
    scale_first = jnp.exp(max_first - new_max)
    scale_second = jnp.exp(max_second - new_max)
    new_total = total_first * scale_first + total_second * scale_second
    new_sum = sum_first * scale_first[..., None] + sum_second * scale_second[..., None]
    return (new_max, new_total, new_sum)


def shards(
    q_prefill,
    k_prefill,
    v_prefill,
    pair_lengths,
    q_decode,
    cache_k,
    cache_v,
    cache_lengths,
    stream,
    out_weight,
    norm_gain,
    vocab_table,
    verdict_ids,
):
    tokens = q_prefill.shape[0]
    seq_index = lax.axis_index("seq")
    kv_local = k_prefill.shape[1] // HD
    group_size = H // KVH
    score_scale = 1.0 / HD**0.5
    pair_ends = jnp.cumsum(pair_lengths)
    query_first = seq_index * tokens
    query_pos = query_first + jnp.arange(tokens, dtype=jnp.int32)
    query_seg = segment_of(query_pos, pair_ends)
    queries = q_prefill.reshape(tokens, kv_local, group_size, HD)

    def attend(state_now, key_block, value_block, first_row):
        key_count = key_block.shape[0]
        key_pos = first_row + jnp.arange(key_count, dtype=jnp.int32)
        key_seg = segment_of(key_pos, pair_ends)
        visible = (
            (query_seg[:, None] == key_seg[None, :])
            & (key_pos[None, :] <= query_pos[:, None])
            & (key_pos[None, :] >= 0)
        )
        row_max, row_total, weighted = state_now
        scores = (
            jnp.einsum(
                "qkgd,nkd->kgqn",
                queries,
                key_block.reshape(key_count, kv_local, HD),
                preferred_element_type=jnp.float32,
            )
            * score_scale
        )
        scores = jnp.where(visible, scores, masked_score)
        new_max = jnp.maximum(row_max, jnp.max(scores, axis=-1))
        exp_terms = jnp.where(visible, jnp.exp(scores - new_max[..., None]), 0.0)
        rescale = jnp.exp(row_max - new_max)
        new_total = row_total * rescale + jnp.sum(exp_terms, axis=-1)
        new_weighted = weighted * rescale[..., None] + jnp.einsum(
            "kgqn,nkd->kgqd",
            exp_terms.astype(jnp.bfloat16),
            value_block.reshape(key_count, kv_local, HD),
            preferred_element_type=jnp.float32,
        )
        return (new_max, new_total, new_weighted)

    def attend_all(state_now, key_rows, value_rows, first_row):
        row_count = key_rows.shape[0]
        block_len = block_rows(row_count, tokens)
        if block_len == row_count:
            return attend(state_now, key_rows, value_rows, first_row)
        block_count = row_count // block_len
        stacked = (
            key_rows.reshape(block_count, block_len, key_rows.shape[1]),
            value_rows.reshape(block_count, block_len, value_rows.shape[1]),
            first_row + block_len * jnp.arange(block_count, dtype=jnp.int32),
        )

        def scan_step(state_in, pieces):
            return (attend(state_in, pieces[0], pieces[1], pieces[2]), None)

        state_out, unused = lax.scan(scan_step, state_now, stacked)
        return state_out

    initial = (
        jnp.full((kv_local, group_size, tokens), masked_score, jnp.float32),
        jnp.zeros((kv_local, group_size, tokens), jnp.float32),
        jnp.zeros((kv_local, group_size, tokens, HD), jnp.float32),
    )
    pieces = (
        lax.all_gather(k_prefill, "seq", axis=0, tiled=True),
        lax.all_gather(v_prefill, "seq", axis=0, tiled=True),
    )
    state_now = attend_all(initial, pieces[0], pieces[1], jnp.int32(0))
    final_max, final_total, final_weighted = state_now
    attended_f = final_weighted / final_total[..., None]
    attended = (
        jnp.transpose(attended_f, (2, 0, 1, 3))
        .reshape(tokens, kv_local * group_size * HD)
        .astype(jnp.bfloat16)
    )
    local_ends = pair_ends - 1 - query_first
    selector = (local_ends[:, None] == jnp.arange(tokens, dtype=jnp.int32)[None, :]).astype(
        jnp.bfloat16
    )
    picked = jnp.dot(selector, attended, preferred_element_type=jnp.float32)
    pair_rows = lax.psum(picked.astype(jnp.bfloat16), "seq")
    cache_count = cache_k.shape[1]
    cache_pos = seq_index * cache_count + jnp.arange(cache_count, dtype=jnp.int32)
    valid = (cache_pos[None, :] < cache_lengths[:, None])[:, None, None, :]
    dec_queries = q_decode.reshape(PROMPTS, kv_local, group_size, HD)
    dec_scores = (
        jnp.einsum(
            "pkgd,pckd->pkgc",
            dec_queries,
            cache_k.reshape(PROMPTS, cache_count, kv_local, HD),
            preferred_element_type=jnp.float32,
        )
        * score_scale
    )
    dec_scores = jnp.where(valid, dec_scores, masked_score)
    dec_max = jnp.max(dec_scores, axis=-1)
    dec_exp = jnp.where(valid, jnp.exp(dec_scores - dec_max[..., None]), 0.0)
    dec_total = jnp.sum(dec_exp, axis=-1)
    dec_sum = jnp.einsum(
        "pkgc,pckd->pkgd",
        dec_exp.astype(jnp.bfloat16),
        cache_v.reshape(PROMPTS, cache_count, kv_local, HD),
        preferred_element_type=jnp.float32,
    )
    dec_max, dec_total, dec_sum = joined((dec_max, dec_total, dec_sum), "seq", merge_partials)
    decode_out = (
        (dec_sum / dec_total[..., None])
        .reshape(PROMPTS, kv_local * group_size * HD)
        .astype(jnp.bfloat16)
    )
    verdict_in = jnp.concatenate([pair_rows, decode_out], axis=0)
    partial_value = jnp.dot(verdict_in, out_weight, preferred_element_type=jnp.float32)
    residual = stream.astype(jnp.float32) + lax.psum(partial_value, "tp")
    squares = jnp.sum(residual * residual, axis=1)
    gained = residual * norm_gain.astype(jnp.float32)[None, :]
    vocab_rows = vocab_table.shape[0]
    local_ids = verdict_ids - lax.axis_index("tp") * vocab_rows
    inside = ((local_ids >= 0) & (local_ids < vocab_rows)).astype(jnp.float32)
    table_rows = vocab_table[jnp.clip(local_ids, 0, vocab_rows - 1)].astype(jnp.float32)
    raw_logits = jnp.sum(gained[:, None, :] * table_rows, axis=2) * inside
    own_squares = squares * (lax.axis_index("tp") == 0).astype(jnp.float32)
    total_squares, raw_total = lax.psum((own_squares, raw_logits), ("seq", "tp"))
    inv_rms = 1.0 / jnp.sqrt(total_squares / D + norm_eps)
    verdict_logits = raw_total * inv_rms[:, None]
    verdict_hidden = (gained * inv_rms[:, None]).astype(jnp.bfloat16)
    win = 1.0 / (1.0 + jnp.exp(verdict_logits[:, 1] - verdict_logits[:, 0]))
    return (attended, verdict_hidden, win)


def solution(mesh):
    placed = (
        P(("groups", "seq"), "tp"),
        P(("groups", "seq"), "tp"),
        P(("groups", "seq"), "tp"),
        P("groups"),
        P("groups", "tp"),
        P("groups", "seq", "tp"),
        P("groups", "seq", "tp"),
        P("groups"),
        P("groups", "seq"),
        P("tp", "seq"),
        P("seq"),
        P("tp", "seq"),
        P("groups", None),
    )
    return jax.shard_map(
        shards,
        mesh=mesh,
        in_specs=placed,
        out_specs=(P(("groups", "seq"), "tp"), P("groups", "seq"), P("groups")),
        check_vma=False,
    )
```

profile of v0, /device:TPU:0, one launch (start us, length us, event | category | flops | bytes accessed | tf_op | source)
XLA Modules:
  0.0 194.4 jit_solution(16273370988699643285)
XLA Ops:
  7.2 0.7 reshape.114
  8.0 0.7 broadcast_compare_fusion
  8.7 1.1 fusion.48
  10.1 14.9 %all-gather.2 = f32[16,2,4,128]{3,2,1,0:T(4,128)S(1)} all-gather(f32[4,2,4,128]{3,2,1,0:T(4,128)S(1)} %fusion.21), channel_id=4, replica_groups=mesh['groups'=2,'seq'=4,'tp'=4] {'seq'}, dimensions={0}, use_global_device_ids=true | all-gather | bytes 81920 | tf_op jit(solution)/shard_map/all_gather | solution.py:18
  25.2 13.2 %all-gather.1 = f32[16,2,4]{2,1,0:T(2,128)S(1)} all-gather(f32[4,2,4]{2,1,0:T(2,128)S(1)} %fusion.32), channel_id=3, replica_groups=mesh['groups'=2,'seq'=4,'tp'=4] {'seq'}, dimensions={0}, use_global_device_ids=true | all-gather | bytes 640 | tf_op jit(solution)/shard_map/all_gather | solution.py:18
  38.4 13.2 %all-gather = f32[16,2,4]{2,1,0:T(2,128)S(1)} all-gather(f32[4,2,4]{2,1,0:T(2,128)S(1)} %get-tuple-element.119), channel_id=2, replica_groups=mesh['groups'=2,'seq'=4,'tp'=4] {'seq'}, dimensions={0}, use_global_device_ids=true | all-gather | bytes 640 | tf_op jit(solution)/shard_map/all_gather | solution.py:18
  51.6 0.8 reduce-window.7
  52.6 1.0 copy.66
  53.6 14.8 %all_gather.24 = bf16[1024,256]{0,1:T(8,128)(2,1)S(1)} all-gather(bf16[256,256]{0,1:T(8,128)(2,1)S(1)} %copy.66), channel_id=1, replica_groups=mesh['groups'=2,'seq'=4,'tp'=4] {'seq'}, dimensions={0}, use_global_device_ids=true | all-gather | bytes 655360 | tf_op jit(solution)/shard_map/all_gather | solution.py:128
  68.4 1.4 reshape.112
  70.1 1.6 fusion.3
  71.7 3.2 %copy-done.2 = f32[2,1024,256,4]{2,1,3,0:T(8,128)} copy-done((f32[2,1024,256,4]{2,1,3,0:T(8,128)}, f32[2,1024,256,4]{2,1,3,0:T(8,128)S(1)}, u32[]{:S(2)}) %copy-start.2) | copy-done | bytes 8388632
  74.9 2.0 %fusion.4 = f32[2,4,256]{2,1,0:T(4,128)S(1)} fusion(f32[2,1024,256,4]{2,1,3,0:T(8,128)S(1)} %get-tuple-element.118, f32[2,4,256]{2,1,0:T(4,128)S(1)} %get-tuple-element.116, pred[256,1024]{0,1:T(8,128)(4,1)S(1)} %fusion.16), kind=kLoop, calls=%fused_computation.12 | loop fusion | flops 10483712 | bytes 8667136 | tf_op jit(solution)/shard_map/reduce_sum | solution.py:95
  76.9 14.7 %all_gather.25 = bf16[1024,256]{1,0:T(8,128)(2,1)S(1)} all-gather(bf16[256,256]{1,0:T(8,128)(2,1)S(1)} %copy-done.3), channel_id=1, replica_groups=mesh['groups'=2,'seq'=4,'tp'=4] {'seq'}, dimensions={0}, use_global_device_ids=true | all-gather | bytes 655360 | tf_op jit(solution)/shard_map/all_gather | solution.py:129
  91.9 5.7 %divide_convert_fusion = bf16[256,2,4,128]{0,3,2,1:T(8,128)(2,1)S(1)} fusion(bf16[1024,2,128,1]{0,2,3,1:T(8,128)(2,1)S(1)} %bitcast.89, f32[2,1024,256,4]{2,1,3,0:T(8,128)} %copy-done.2, f32[2,4,256]{2,1,0:T(4,128)S(1)} %get-tuple-element.116, pred[256,1024]{0,1:T(8,128)(4,1)S(1)} %fusion.16, f32[256,2,4]{0,2,1:T(4,128)S(1)} %bitcast_add_fusion, ...), kind=kOutput, calls=%fused_computation.21 | convolution fusion | flops 548143104 | bytes 9723904 | tf_op jit(solution)/shard_map/kgqn,nkd->kgqd/dot_general | solution.py:96
  97.8 19.3 %psum.28 = bf16[8,1024]{1,0:T(8,128)(2,1)S(1)} all-reduce(bf16[8,1024]{1,0:T(8,128)(2,1)S(1)} %convolution_convert_fusion), channel_id=1, replica_groups=mesh['groups'=2,'seq'=4,'tp'=4] {'seq'}, use_global_device_ids=true, to_apply=%region_5.6 | all-reduce | flops 8192 | bytes 32768 | tf_op jit(solution)/shard_map/psum | solution.py:144
  117.7 3.5 %fusion.27 = f32[12,2048]{1,0:T(8,128)} fusion(bf16[1024,2048]{1,0:T(8,128)(2,1)} %param.24, bf16[4,1024]{1,0:T(4,128)(2,1)S(1)} %convert_element_type.53, bf16[8,1024]{1,0:T(8,128)(2,1)S(1)} %psum.28), kind=kOutput, calls=%fused_computation.36 | convolution fusion | flops 50380800 | bytes 4317184 | tf_op jit(solution)/shard_map/dot_general | solution.py:175
  121.5 2.2 %gather_fusion = bf16[24,2048]{1,0:T(8,128)(2,1)S(1)} fusion(bf16[16032,2048]{1,0:T(8,128)(2,1)} %param.26, s32[1024]{0:T(1024)S(1)} %pad_clamp_fusion), kind=kCustom, calls=%fused_computation | custom fusion | bytes 196704 | tf_op jit(solution)/shard_map/gather | solution.py:182
  123.8 27.5 %all-reduce.3.cloned.1.call-done = f32[12,2048]{1,0:T(8,128)} async-done(((f32[12,2048]{1,0:T(8,128)}), f32[12,2048]{1,0:T(8,128)}) %all-reduce.3.cloned.1.call-update) | async-done | bytes 98320 | tf_op jit(solution)/shard_map/psum | solution.py:176
  151.4 1.0 multiply_reduce_fusion.1
  152.6 1.0 copy.78
  153.6 32.4 %all-reduce = (f32[12]{0:T(128)S(1)}, f32[12,2]{1,0:T(8,128)S(1)}) all-reduce(f32[12]{0:T(128)S(1)} %broadcast_multiply_fusion.1, f32[12,2]{1,0:T(8,128)S(1)} %and_select_fusion), channel_id=1, replica_groups=mesh['groups'=2,'seq'=4,'tp'=4] {'seq','tp'}, use_global_device_ids=true, to_apply=%region_12.13 | all-reduce | flops 36 | bytes 288 | tf_op jit(solution)/shard_map/psum | solution.py:185
  186.0 0.7 multiply_convert_fusion
  186.8 0.7 fusion.39
  (53 shorter events, 2.9 us)
Async XLA Ops:
  7.2 2.7 %copy-start = (bf16[4,64,256]{2,1,0:T(8,128)(2,1)S(1)}, bf16[4,64,256]{2,1,0:T(8,128)(2,1)}, u32[]{:S(2)}) copy-start(bf16[4,64,256]{2,1,0:T(8,128)(2,1)} %param.21) | copy-start | bytes 393220
  7.2 144.2 %all-reduce.3.cloned.1.call-start = ((), (), s32[]{:S(2)}) async-start(), calls=%async_computation | async-start | bytes 262144 | tf_op jit(solution)/shard_map/psum | solution.py:176
  70.1 6.9 %copy-start.3 = (bf16[256,256]{1,0:T(8,128)(2,1)S(1)}, bf16[256,256]{1,0:T(8,128)(2,1)}, u32[]{:S(2)}) copy-start(bf16[256,256]{1,0:T(8,128)(2,1)} %param.17) | copy-start | bytes 393220
  71.7 3.2 %copy-start.2 = (f32[2,1024,256,4]{2,1,3,0:T(8,128)}, f32[2,1024,256,4]{2,1,3,0:T(8,128)S(1)}, u32[]{:S(2)}) copy-start(f32[2,1024,256,4]{2,1,3,0:T(8,128)S(1)} %get-tuple-element.118) | copy-start | bytes 25165828
  91.8 29.4 %copy-start.6 = (s32[12,2]{0,1:T(2,128)S(1)}, s32[12,2]{0,1:T(2,128)}, u32[]{:S(2)}) copy-start(s32[12,2]{0,1:T(2,128)} %param.27) | copy-start | bytes 292
  91.9 29.6 %copy-start.5 = (bf16[2048]{0:T(1024)(128)(2,1)S(1)}, bf16[2048]{0:T(1024)(128)(2,1)}, u32[]{:S(2)}) copy-start(bf16[2048]{0:T(1024)(128)(2,1)} %param.25) | copy-start | bytes 12292
  91.9 59.5 %copy-start.4 = (bf16[12,2048]{1,0:T(8,128)(2,1)S(1)}, bf16[12,2048]{1,0:T(8,128)(2,1)}, u32[]{:S(2)}) copy-start(bf16[12,2048]{1,0:T(8,128)(2,1)} %param.23) | copy-start | bytes 147460
  91.9 95.6 %copy-start.1 = (bf16[4,64,256]{2,1,0:T(8,128)(2,1)S(1)}, bf16[4,64,256]{2,1,0:T(8,128)(2,1)}, u32[]{:S(2)}) copy-start(bf16[4,64,256]{2,1,0:T(8,128)(2,1)} %param.21) | copy-start | bytes 393220
Sparse Core Ops, SparseCore 0:
  121.4 29.9 all-reduce.2
where the time goes:
time: 195 us; the launch traced here: 194 us
  blocking collectives  123 us (63%)
  waiting for transfers between devices  27.6 us (14%)
  between operations  14.3 us (7%)
  matrix products  12.4 us (6%)
  local copies, waits for them, and re-layouts  10.1 us (5%)
  other arithmetic  7.42 us (4%)
    all_gather x3, blocking collectives, joined(): pieces = jax.tree.map(lambda part: lax.all_gather(part, axis), value)  41.4 us
    psum x1, blocking collectives, shards(): lax.psum((own_squares, raw_logits), ('seq', 'tp'))  32.4 us
    psum x1, waiting for transfers between devices, shards(): residual = stream.astype(jnp.float32) + lax.psum(partial_value, 'tp')  27.5 us
    psum x1, blocking collectives, shards(): pair_rows = lax.psum(picked.astype(jnp.bfloat16), 'seq')  19.3 us
    all_gather x1, blocking collectives, shards(): lax.all_gather(k_prefill, 'seq', axis=0, tiled=True)  14.8 us
    all_gather x1, blocking collectives, shards(): lax.all_gather(v_prefill, 'seq', axis=0, tiled=True)  14.7 us
    dot_general x1, matrix products, attend(): jnp.einsum('kgqn,nkd->kgqd', exp_terms.astype(jnp.bfloat16), value_block....  5.71 us
    unnamed x17, local copies, waits for them, and re-layouts  5.34 us
  transfers between devices with their start and end apart: 1, of which 1 were waited for; matrix products, arithmetic and copies ran while one was open for 1% of the time, Pallas kernels for 0%

commit v1 on v0

v1 whole, which is shorter than its diff:
```python
import functools
import math

import jax
import jax.numpy as jnp
from jax import lax
from jax.experimental import pallas as pl
from jax.experimental.pallas import tpu as pltpu
from jax.sharding import PartitionSpec as P

HD = 128
ROW = 8
MASKED = -1e30
EPS = 1e-05
BF = jnp.bfloat16
F32 = jnp.float32
MESH = pl.DeviceIdType.MESH


def up(value, step):
    return -(-value // step) * step


def dot(a, b, dims):
    return lax.dot_general(a, b, (dims, ((), ())), preferred_element_type=F32)


def kernel(
    ns, nt, width, spans,
    len_ref, clen_ref, q_ref, k_ref, v_ref, qd_ref, ck_ref, cv_ref, stream_ref, gain_ref, tbl_ref, w_ref,
    att_ref, hid_ref, win_ref,
    kbuf, vbuf, bias, mrow, lrow, acc, qdpad, qsel, qx, pout, pstat, pox, psx, wbuf, part, partx, tblx, stat, statx,
    ks, kr, vs, vr, qs, qr, pos, por, pss, psr, ts, tr, gs, gr, ss, sr, wsem,
):
    me = lax.axis_index("seq")
    mt = lax.axis_index("tp")
    tokens = q_ref.shape[0]
    heads = q_ref.shape[1] // HD
    kvl = k_ref.shape[1] // HD
    group = heads // kvl
    pairs = len_ref.shape[0]
    prompts, cache_n = ck_ref.shape[0], ck_ref.shape[1]
    scale2 = math.log2(math.e) / HD**0.5
    reach = len(spans)
    cols = pstat.shape[1]

    def head(h):
        return slice(h * HD, (h + 1) * HD)

    def relay(d, keys):
        src, buf, send, recv = (k_ref, kbuf, ks, kr) if keys else (v_ref, vbuf, vs, vr)
        low = spans[d - 1]
        rows = pl.ds(low, tokens - low)
        block = src.at[rows] if d == 1 else buf.at[d - 2, rows]
        return pltpu.make_async_remote_copy(
            src_ref=block,
            dst_ref=buf.at[d - 1, rows],
            send_sem=send.at[d - 1],
            recv_sem=recv.at[d - 1],
            device_id={"seq": lax.rem(me + 1, ns)},
            device_id_type=MESH,
        )

    def sends(d):
        return (me < ns - 1) & (me >= d - 1)

    def exchange(src, dst, send, recv, axis, mine, count):
        return [
            pltpu.make_async_remote_copy(
                src_ref=src,
                dst_ref=dst.at[mine],
                send_sem=send.at[d - 1],
                recv_sem=recv.at[d - 1],
                device_id={axis: lax.rem(mine + d, count)},
                device_id_type=MESH,
            )
            for d in range(1, count)
        ]

    weight_copy = pltpu.make_async_copy(w_ref, wbuf, wsem)
    weight_copy.start()
    barrier = pltpu.get_barrier_semaphore()
    for d in range(1, ns):
        pl.semaphore_signal(barrier, inc=1, device_id={"seq": lax.rem(me + d, ns)}, device_id_type=MESH)
    for d in range(1, nt):
        pl.semaphore_signal(barrier, inc=1, device_id={"tp": lax.rem(mt + d, nt)}, device_id_type=MESH)

    ends, total = [], jnp.int32(0)
    for p in range(pairs):
        total = total + len_ref[p]
        ends.append(total)
    starts = [jnp.int32(0)] + ends[:-1]
    first = me * tokens
    row_p = lax.broadcasted_iota(jnp.int32, (ROW, tokens), 0)
    last = jnp.full((ROW, tokens), -1, jnp.int32)
    for p in range(pairs):
        last = jnp.where(row_p == p, ends[p] - 1 - first, last)
    chosen = (lax.broadcasted_iota(jnp.int32, (ROW, tokens), 1) == last).astype(F32).astype(BF)
    picked = dot(chosen, q_ref[...], ((1,), (0,)))
    qsel[...] = picked.astype(BF)

    if ns + nt > 2:
        pl.semaphore_wait(barrier, ns + nt - 2)
    if reach:
        @pl.when(sends(1))
        def _():
            relay(1, True).start()

    q_moves = exchange(qsel, qx, qs, qr, "seq", me, ns)
    for move in q_moves:
        move.start()
    if reach:
        @pl.when(sends(1))
        def _():
            relay(1, False).start()

    t_moves = exchange(tbl_ref, tblx, gs, gr, "tp", mt, nt)
    for move in t_moves:
        move.start()

    q_pos = lax.broadcasted_iota(jnp.int32, (tokens, tokens), 1)
    k_pos = lax.broadcasted_iota(jnp.int32, (tokens, tokens), 0)
    seg_start = jnp.zeros((1, tokens), jnp.int32)
    q_row = lax.broadcasted_iota(jnp.int32, (1, tokens), 1) + first
    for p in range(pairs):
        seg_start = jnp.where(ends[p] <= q_row, ends[p], seg_start)
    seg_local = seg_start - first

    def attend(d, low):
        count = tokens - low
        if d == 0:
            visible = (k_pos >= seg_local) & (k_pos <= q_pos)
        else:
            visible = k_pos[:count] + (low - d * tokens) >= seg_local
        bias[:count, :] = jnp.where(visible, 0.0, MASKED)
        for kv in range(kvl):
            if d == 0:
                keys, values = k_ref[:, head(kv)], v_ref[:, head(kv)]
            else:
                keys, values = kbuf[d - 1, low:, head(kv)], vbuf[d - 1, low:, head(kv)]
            values_t = values.T
            for g in range(group):
                h = kv * group + g
                s = dot(keys, q_ref[:, head(h)], ((1,), (1,))) + bias[:count, :]
                top = jnp.max(s, axis=0, keepdims=True)
                if d:
                    old = mrow[h : h + 1, :]
                    top = jnp.maximum(top, old)
                p = jnp.exp2((s - top) * scale2)
                weighted = dot(values_t, p.astype(BF), ((1,), (0,)))
                summed = jnp.sum(p, axis=0, keepdims=True)
                if d:
                    keep = jnp.exp2((old - top) * scale2)
                    summed = summed + lrow[h : h + 1, :] * keep
                    weighted = weighted + acc[h] * keep
                mrow[h : h + 1, :] = top
                lrow[h : h + 1, :] = summed
                acc[h] = weighted

    def step(d):
        @pl.when(me >= d)
        def _():
            relay(d, True).wait_recv()
            if d < reach:
                @pl.when(sends(d + 1))
                def _():
                    relay(d + 1, True).start()
            relay(d, False).wait_recv()
            if d < reach:
                @pl.when(sends(d + 1))
                def _():
                    relay(d + 1, False).start()
            attend(d, spans[d - 1])

    attend(0, 0)

    for move in q_moves:
        move.wait_recv()
    q_pair = qsel[...].astype(F32)
    for d in range(1, ns):
        q_pair = q_pair + qx[lax.rem(me + d, ns)].astype(F32)
    qdpad[...] = jnp.zeros_like(qdpad)
    qdpad[:prompts, :] = qd_ref[...].astype(F32)
    q_dec = qdpad[...]
    pieces = [side[:, head(h)] for side in (q_pair, q_dec) for h in range(heads)]
    used = 2 * heads * ROW
    if cols > used:
        pieces.append(jnp.zeros((cols - used, HD), F32))
    q_cols = jnp.concatenate(pieces, axis=0).astype(BF)

    col = lax.broadcasted_iota(jnp.int32, (1, cols), 1)
    col_row = lax.rem(col, ROW)
    low_pair, high_pair = jnp.zeros((1, cols), jnp.int32), jnp.zeros((1, cols), jnp.int32)
    low_dec, high_dec = low_pair, high_pair
    for p in range(pairs):
        low_pair = jnp.where(col_row == p, starts[p] - first, low_pair)
        high_pair = jnp.where(col_row == p, ends[p] - first, high_pair)
    for p in range(prompts):
        ours = jnp.minimum(jnp.maximum(clen_ref[p] - me * cache_n, 0), cache_n)
        low_dec = jnp.where(col_row == p, p * cache_n, low_dec)
        high_dec = jnp.where(col_row == p, p * cache_n + ours, high_dec)

    blocks = []
    for kind in range(2):
        for kv in range(kvl):
            if kind == 0:
                keys, values = k_ref[:, head(kv)], v_ref[:, head(kv)]
                low_j, high_j = low_pair, high_pair
            else:
                keys = ck_ref[:, :, head(kv)].reshape(prompts * cache_n, HD)
                values = cv_ref[:, :, head(kv)].reshape(prompts * cache_n, HD)
                low_j, high_j = low_dec, high_dec
            begin = (kind * heads + kv * group) * ROW
            inside = (col >= begin) & (col < begin + group * ROW)
            high_j = jnp.where(inside, high_j, low_j)
            index = lax.broadcasted_iota(jnp.int32, (keys.shape[0], cols), 0)
            visible = (index >= low_j) & (index < high_j)
            s = jnp.where(visible, dot(keys, q_cols, ((1,), (1,))), MASKED)
            blocks.append((visible, s, values))
    top = functools.reduce(jnp.maximum, [jnp.max(s, axis=0, keepdims=True) for _, s, _ in blocks])
    p_sum = jnp.zeros((1, cols), F32)
    p_out = jnp.zeros((HD, cols), F32)
    for visible, s, values in blocks:
        p = jnp.where(visible, jnp.exp2((s - top) * scale2), 0.0)
        p_sum = p_sum + jnp.sum(p, axis=0, keepdims=True)
        p_out = p_out + dot(values.T, p.astype(BF), ((1,), (0,)))
    pout[...] = p_out.astype(BF)
    stat_row = lax.broadcasted_iota(jnp.int32, (ROW, cols), 0)
    pstat[...] = jnp.where(stat_row == 0, top, p_sum)
    o_moves = exchange(pout, pox, pos, por, "seq", me, ns)
    s_moves = exchange(pstat, psx, pss, psr, "seq", me, ns)
    for move, other in zip(o_moves, s_moves):
        move.start()
        other.start()
    pox[me] = pout[...]
    psx[me] = pstat[...]

    if reach:
        step(1)

    for move, other in zip(o_moves, s_moves):
        move.wait_recv()
        other.wait_recv()
    top = psx[0, 0:1, :]
    for i in range(1, ns):
        top = jnp.maximum(top, psx[i, 0:1, :])
    p_sum = jnp.zeros((1, cols), F32)
    p_out = jnp.zeros((HD, cols), F32)
    for i in range(ns):
        keep = jnp.exp2((psx[i, 0:1, :] - top) * scale2)
        p_sum = p_sum + psx[i, 1:2, :] * keep
        p_out = p_out + pox[i].astype(F32) * keep
    rows_t = (p_out / jnp.where(p_sum > 0.0, p_sum, 1.0)).T
    sides = [
        jnp.concatenate([rows_t[(kind * heads + h) * ROW : (kind * heads + h + 1) * ROW, :] for h in range(heads)], axis=1)
        for kind in range(2)
    ]
    verdict_in = jnp.concatenate(sides, axis=0).astype(BF)
    weight_copy.wait()
    part[...] = dot(verdict_in, wbuf[...], ((1,), (0,))).astype(BF)
    a_moves = exchange(part, partx, ts, tr, "tp", mt, nt)
    for move in a_moves:
        move.start()
    partx[mt] = part[...]
    tblx[mt] = tbl_ref[...]

    if reach > 1:
        step(2)

    for move in t_moves + a_moves:
        move.wait_recv()
    rows = stream_ref.shape[0]
    table = tblx[0].astype(F32)
    added = partx[0].astype(F32)
    for i in range(1, nt):
        table = table + tblx[i].astype(F32)
        added = added + partx[i].astype(F32)
    half = table.shape[0] // 2
    residual = stream_ref[...].astype(F32) + jnp.concatenate([added[:pairs], added[ROW : ROW + prompts]], axis=0)
    gained = residual * gain_ref[...].astype(F32)
    squares = jnp.sum(residual * residual, axis=1, keepdims=True)
    raw0 = jnp.sum(gained * table[:rows], axis=1, keepdims=True)
    raw1 = jnp.sum(gained * table[half : half + rows], axis=1, keepdims=True)
    lane = lax.broadcasted_iota(jnp.int32, stat.shape, 1)
    stat[...] = jnp.where(lane == 0, squares, jnp.where(lane == 1, raw0, raw1))
    f_moves = exchange(stat, statx, ss, sr, "seq", me, ns)
    for move in f_moves:
        move.start()
    statx[me] = stat[...]

    for d in range(3, reach + 1):
        step(d)

    for h in range(heads):
        att_ref[:, head(h)] = (acc[h] / lrow[h : h + 1, :]).T.astype(BF)

    for move in f_moves:
        move.wait_recv()
    sums = statx[0]
    for i in range(1, ns):
        sums = sums + statx[i]
    inv = 1.0 / jnp.sqrt(sums[:, 0:1] / width + EPS)
    hid_ref[...] = (gained * inv).astype(BF)
    win = 1.0 / (1.0 + jnp.exp(sums[:, 2:3] * inv - sums[:, 1:2] * inv))
    win_ref[...] = jnp.broadcast_to(win, win_ref.shape)

    for d in range(1, reach + 1):
        @pl.when(sends(d))
        def _():
            relay(d, True).wait_send()
            relay(d, False).wait_send()
    for move in q_moves + t_moves + o_moves + s_moves + a_moves + f_moves:
        move.wait_send()


def shards(
    ns, nt, width,
    q_prefill, k_prefill, v_prefill, pair_lengths, q_decode, cache_k, cache_v, cache_lengths,
    stream, out_weight, norm_gain, vocab_table, verdict_ids,
):
    tokens, kv_width = k_prefill.shape
    heads = q_prefill.shape[1] // HD
    rows, columns = stream.shape
    most = tokens * ns * 5 // 8
    spans = []
    for d in range(1, ns):
        low = max(0, d * tokens - most + 1)
        if low < tokens:
            spans.append(low // 128 * 128)
    reach = len(spans)
    slots = max(reach, 1)
    cols = up(2 * heads * ROW, 128)
    half = up(rows, 16)

    ids = jnp.full((2, half), -1, jnp.int32).at[:, :rows].set(verdict_ids.T).reshape(-1)
    vocab_rows = vocab_table.shape[0]
    local_ids = ids - jnp.where(ids >= 0, lax.axis_index("tp") * vocab_rows, 0)
    inside = (local_ids >= 0) & (local_ids < vocab_rows)
    table = vocab_table[jnp.clip(local_ids, 0, vocab_rows - 1)]
    table = jnp.where(inside[:, None], table, jnp.zeros_like(table))

    vmem = pl.BlockSpec(memory_space=pltpu.VMEM)
    smem = pl.BlockSpec(memory_space=pltpu.SMEM)
    peers_s, peers_t = max(ns - 1, 1), max(nt - 1, 1)
    dma = pltpu.SemaphoreType.DMA
    attended, hidden, win = pl.pallas_call(
        functools.partial(kernel, ns, nt, width, tuple(spans)),
        out_shape=(
            jax.ShapeDtypeStruct(q_prefill.shape, BF),
            jax.ShapeDtypeStruct(stream.shape, BF),
            jax.ShapeDtypeStruct((rows, 128), F32),
        ),
        in_specs=[smem, smem] + [vmem] * 9 + [pl.BlockSpec(memory_space=pl.ANY)],
        out_specs=(vmem, vmem, vmem),
        scratch_shapes=[
            pltpu.VMEM((slots, tokens, kv_width), BF),
            pltpu.VMEM((slots, tokens, kv_width), BF),
            pltpu.VMEM((tokens, tokens), F32),
            pltpu.VMEM((heads, tokens), F32),
            pltpu.VMEM((heads, tokens), F32),
            pltpu.VMEM((heads, HD, tokens), F32),
            pltpu.VMEM((ROW, heads * HD), F32),
            pltpu.VMEM((ROW, heads * HD), BF),
            pltpu.VMEM((ns, ROW, heads * HD), BF),
            pltpu.VMEM((HD, cols), BF),
            pltpu.VMEM((ROW, cols), F32),
            pltpu.VMEM((ns, HD, cols), BF),
            pltpu.VMEM((ns, ROW, cols), F32),
            pltpu.VMEM(out_weight.shape, BF),
            pltpu.VMEM((2 * ROW, columns), BF),
            pltpu.VMEM((nt, 2 * ROW, columns), BF),
            pltpu.VMEM((nt, 2 * half, columns), BF),
            pltpu.VMEM((rows, 128), F32),
            pltpu.VMEM((ns, rows, 128), F32),
            dma((slots,)), dma((slots,)), dma((slots,)), dma((slots,)),
            dma((peers_s,)), dma((peers_s,)),
            dma((peers_s,)), dma((peers_s,)),
            dma((peers_s,)), dma((peers_s,)),
            dma((peers_t,)), dma((peers_t,)),
            dma((peers_t,)), dma((peers_t,)),
            dma((peers_s,)), dma((peers_s,)),
            dma,
        ],
        compiler_params=pltpu.CompilerParams(
            collective_id=0, has_side_effects=True, vmem_limit_bytes=48 * 1024 * 1024
        ),
    )(
        pair_lengths, cache_lengths, q_prefill, k_prefill, v_prefill, q_decode, cache_k, cache_v,
        stream, norm_gain.reshape(1, columns), table, out_weight,
    )
    return attended, hidden, win[:, 0]


def solution(mesh):
    placed = (
        P(("groups", "seq"), "tp"),
        P(("groups", "seq"), "tp"),
        P(("groups", "seq"), "tp"),
        P("groups"),
        P("groups", "tp"),
        P("groups", "seq", "tp"),
        P("groups", "seq", "tp"),
        P("groups"),
        P("groups", "seq"),
        P("tp", "seq"),
        P("seq"),
        P("tp", "seq"),
        P("groups", None),
    )
    ns, nt = mesh.shape["seq"], mesh.shape["tp"]

    def body(*args):
        return shards(ns, nt, args[8].shape[1] * ns, *args)

    return jax.shard_map(
        body,
        mesh=mesh,
        in_specs=placed,
        out_specs=(P(("groups", "seq"), "tp"), P("groups", "seq"), P("groups")),
        check_vma=False,
    )
```

time: 195 us -> 47.6 us (0.24)
  blocking collectives: 123 us -> 0 us
  Pallas kernels: 0 us -> 29.4 us
  waiting for transfers between devices: 27.6 us -> 0 us
  between operations: 14.3 us -> 0.67 us
  matrix products: 12.4 us -> 0 us
  other arithmetic: 7.42 us -> 2.08 us
  local copies, waits for them, and re-layouts: 10.1 us -> 14.9 us
    all_gather x5 -> x0, blocking collectives: 70.8 us -> none  [the longest x3 41.4 us: joined(): pieces = jax.tree.map(lambda part: lax.all_gather(part, axis), value)]
    psum x2 -> x0, blocking collectives: 51.7 us -> none  [the longest x1 32.4 us: shards(): lax.psum((own_squares, raw_logits), ('seq', 'tp'))]
    pallas_call x0 -> x1, Pallas kernels: none -> 29.4 us  [shards(): pl.pallas_call(functools.partial(kernel, ns, nt, width, tuple(spans)), ou...]
    psum x1 -> x0, waiting for transfers between devices: 27.5 us -> none  [shards(): residual = stream.astype(jnp.float32) + lax.psum(partial_value, 'tp')]
    dot_general x6 -> x0, matrix products: 12.4 us -> none  [the longest x1 5.71 us: attend(): jnp.einsum('kgqn,nkd->kgqd', exp_terms.astype(jnp.bfloat16), value_block....]
    unnamed x17 -> x22, local copies, waits for them, and re-layouts: 5.34 us -> 11.1 us
    reduce_sum x6 -> x0, other arithmetic: 3.57 us -> none  [the longest x1 2.02 us: attend(): new_total = row_total * rescale + jnp.sum(exp_terms, axis=-1)]
  transfers between devices with their start and end apart: 1 -> 0, of which waited for: 1 -> 0; matrix products, arithmetic and copies ran while one was open for 1% -> 0% of each run, Pallas kernels for 0% -> 0%
where the time goes in v1:
time: 47.6 us; the launch traced here: 47 us
  Pallas kernels  29.4 us (62%)
  local copies, waits for them, and re-layouts  14.9 us (31%)
  other arithmetic  2.08 us (4%)
  between operations  0.67 us (1%)
    pallas_call x1, Pallas kernels, shards(): pl.pallas_call(functools.partial(kernel, ns, nt, width, tuple(spans)), ou...  29.4 us
    unnamed x22, local copies, waits for them, and re-layouts  11.1 us
    gather x1, local copies, waits for them, and re-layouts, shards(): table = vocab_table[jnp.clip(local_ids, 0, vocab_rows - 1)]  2.28 us
    another operation x2, other arithmetic  1.97 us

profile of v1, /device:TPU:0, one launch (start us, length us, event | category | flops | bytes accessed | tf_op | source)
XLA Modules:
  0.0 47.0 jit_solution(8301139303926168012)
XLA Ops:
  0.6 0.6 %compare_reduce_fusion = pred[]{:T(512)} fusion(), kind=kLoop, calls=%fused_computation.8 | loop fusion | flops 5 | bytes 1 | tf_op jit(solution)/shard_map/reduce.1
  1.3 1.3 %select_bitcast_fusion = s32[2,12]{1,0:T(2,128)S(1)} fusion(s32[12,2]{0,1:T(2,128)} %param.27, pred[]{:T(512)} %compare_reduce_fusion), kind=kLoop, calls=%fused_computation.9 | loop fusion | flops 24 | bytes 193 | tf_op jit(solution)/shard_map/transpose.9
  2.6 0.1 reshape.84
  2.7 0.1 reshape.83
  2.8 0.7 %reshape.82.gain_ref = bf16[1,2048]{1,0:T(2,128)(2,1)S(1)} reshape(bf16[2048]{0:T(1024)(128)(2,1)} %param.25) | data formatting | bytes 8192 | tf_op jit(solution)/shard_map/reshape | solution.py:389
  3.5 2.3 %gather_fusion = bf16[32,2048]{1,0:T(8,128)(2,1)S(1)} fusion(bf16[16032,2048]{1,0:T(8,128)(2,1)} %param.26, s32[1024]{0:T(1024)S(1)} %pad_clamp_fusion), kind=kCustom, calls=%fused_computation | custom fusion | bytes 262272 | tf_op jit(solution)/shard_map/gather | solution.py:339
  5.8 0.1 broadcast_select_fusion.tbl_ref
  5.9 0.0 copy-start
  5.9 2.2 %copy-done = bf16[1024,2048]{1,0:T(8,128)(2,1)S(1)} copy-done((bf16[1024,2048]{1,0:T(8,128)(2,1)S(1)}, bf16[1024,2048]{1,0:T(8,128)(2,1)}, u32[]{:S(2)}) %copy-start) | copy-done | bytes 4194328
  8.1 0.0 copy-start.1
  8.1 1.0 %copy-done.1 = bf16[256,1024]{1,0:T(8,128)(2,1)S(1)} copy-done((bf16[256,1024]{1,0:T(8,128)(2,1)S(1)}, bf16[256,1024]{1,0:T(8,128)(2,1)}, u32[]{:S(2)}) %copy-start.1) | copy-done | bytes 524312
  9.1 0.0 copy-start.2
  9.1 0.9 %copy-done.2 = bf16[256,256]{1,0:T(8,128)(2,1)S(1)} copy-done((bf16[256,256]{1,0:T(8,128)(2,1)S(1)}, bf16[256,256]{1,0:T(8,128)(2,1)}, u32[]{:S(2)}) %copy-start.2) | copy-done | bytes 131096
  10.0 0.9 %copy-done.3 = bf16[256,256]{1,0:T(8,128)(2,1)S(1)} copy-done((bf16[256,256]{1,0:T(8,128)(2,1)S(1)}, bf16[256,256]{1,0:T(8,128)(2,1)}, u32[]{:S(2)}) %copy-start.3) | copy-done | bytes 131096
  10.9 0.9 %copy-done.4 = bf16[4,64,256]{2,1,0:T(8,128)(2,1)S(1)} copy-done((bf16[4,64,256]{2,1,0:T(8,128)(2,1)S(1)}, bf16[4,64,256]{2,1,0:T(8,128)(2,1)}, u32[]{:S(2)}) %copy-start.4) | copy-done | bytes 131096
  11.8 0.9 %copy-done.5 = bf16[4,64,256]{2,1,0:T(8,128)(2,1)S(1)} copy-done((bf16[4,64,256]{2,1,0:T(8,128)(2,1)S(1)}, bf16[4,64,256]{2,1,0:T(8,128)(2,1)}, u32[]{:S(2)}) %copy-start.5) | copy-done | bytes 131096
  12.7 0.8 %copy-done.6 = bf16[12,2048]{1,0:T(8,128)(2,1)S(1)} copy-done((bf16[12,2048]{1,0:T(8,128)(2,1)S(1)}, bf16[12,2048]{1,0:T(8,128)(2,1)}, u32[]{:S(2)}) %copy-start.6) | copy-done | bytes 49176
  13.6 0.7 %copy-done.7 = bf16[4,1024]{1,0:T(4,128)(2,1)S(1)} copy-done((bf16[4,1024]{1,0:T(4,128)(2,1)S(1)}, bf16[4,1024]{1,0:T(4,128)(2,1)}, u32[]{:S(2)}) %copy-start.7) | copy-done | bytes 8216
  14.3 0.7 %copy-done.8 = s32[8]{0:T(128)S(1)} copy-done((s32[8]{0:T(128)S(1)}, s32[8]{0:T(128)}, u32[]{:S(2)}) %copy-start.8) | copy-done | bytes 56
  14.9 0.7 %copy-done.9 = s32[4]{0:T(128)S(1)} copy-done((s32[4]{0:T(128)S(1)}, s32[4]{0:T(128)}, u32[]{:S(2)}) %copy-start.9) | copy-done | bytes 40
  15.6 29.4 %shard_map.148 = (bf16[256,1024]{1,0:T(8,128)(2,1)S(1)}, bf16[12,2048]{1,0:T(8,128)(2,1)S(1)}, f32[12,128]{1,0:T(8,128)S(1)}) custom-call(s32[8]{0:T(128)S(1)} %copy-done.8, s32[4]{0:T(128)S(1)} %copy-done.9, bf16[256,1024]{1,0:T(8,128)(2,1)S(1)} %copy-done.1, bf16[256,256]{1,0:T(8,128)(2,1)S(1)} %copy-done.2, bf16[256,256]{1,0:T(8,128)(2,1)S(1)} %copy-done.3, ...), custom_call_target="tpu_custom_call" | custom-call | tf_op jit(solution)/shard_map/pallas_call | solution.py:346
  45.0 0.6 %slice_reduce_fusion = f32[12]{0:T(128)} fusion(f32[12,128]{1,0:T(8,128)S(1)} %get-tuple-element.20), kind=kLoop, calls=%fused_computation.2 | loop fusion | bytes 96 | tf_op jit(solution)/shard_map/slice | solution.py:391
  45.6 0.8 %copy.18 = bf16[256,1024]{1,0:T(8,128)(2,1)} copy(bf16[256,1024]{1,0:T(8,128)(2,1)S(1)} %get-tuple-element.24) | data formatting | bytes 1048576
  46.4 0.6 %copy.19 = bf16[12,2048]{1,0:T(8,128)(2,1)} copy(bf16[12,2048]{1,0:T(8,128)(2,1)S(1)} %get-tuple-element.25) | data formatting | bytes 98304
  (11 shorter events, 0.0 us)
Async XLA Ops:
  5.9 2.2 %copy-start = (bf16[1024,2048]{1,0:T(8,128)(2,1)S(1)}, bf16[1024,2048]{1,0:T(8,128)(2,1)}, u32[]{:S(2)}) copy-start(bf16[1024,2048]{1,0:T(8,128)(2,1)} %w_ref.1) | copy-start | bytes 12582916
  8.1 1.0 %copy-start.1 = (bf16[256,1024]{1,0:T(8,128)(2,1)S(1)}, bf16[256,1024]{1,0:T(8,128)(2,1)}, u32[]{:S(2)}) copy-start(bf16[256,1024]{1,0:T(8,128)(2,1)} %q_ref.1) | copy-start | bytes 1572868
  9.1 0.9 %copy-start.2 = (bf16[256,256]{1,0:T(8,128)(2,1)S(1)}, bf16[256,256]{1,0:T(8,128)(2,1)}, u32[]{:S(2)}) copy-start(bf16[256,256]{1,0:T(8,128)(2,1)} %k_ref.1) | copy-start | bytes 393220
  10.0 0.9 %copy-start.3 = (bf16[256,256]{1,0:T(8,128)(2,1)S(1)}, bf16[256,256]{1,0:T(8,128)(2,1)}, u32[]{:S(2)}) copy-start(bf16[256,256]{1,0:T(8,128)(2,1)} %v_ref.1) | copy-start | bytes 393220
  10.9 0.9 %copy-start.4 = (bf16[4,64,256]{2,1,0:T(8,128)(2,1)S(1)}, bf16[4,64,256]{2,1,0:T(8,128)(2,1)}, u32[]{:S(2)}) copy-start(bf16[4,64,256]{2,1,0:T(8,128)(2,1)} %ck_ref.1) | copy-start | bytes 393220
  11.8 0.9 %copy-start.5 = (bf16[4,64,256]{2,1,0:T(8,128)(2,1)S(1)}, bf16[4,64,256]{2,1,0:T(8,128)(2,1)}, u32[]{:S(2)}) copy-start(bf16[4,64,256]{2,1,0:T(8,128)(2,1)} %cv_ref.1) | copy-start | bytes 393220
  12.7 0.8 %copy-start.6 = (bf16[12,2048]{1,0:T(8,128)(2,1)S(1)}, bf16[12,2048]{1,0:T(8,128)(2,1)}, u32[]{:S(2)}) copy-start(bf16[12,2048]{1,0:T(8,128)(2,1)} %stream_ref.1) | copy-start | bytes 147460
  13.6 0.7 %copy-start.7 = (bf16[4,1024]{1,0:T(4,128)(2,1)S(1)}, bf16[4,1024]{1,0:T(4,128)(2,1)}, u32[]{:S(2)}) copy-start(bf16[4,1024]{1,0:T(4,128)(2,1)} %qd_ref.1) | copy-start | bytes 24580
  14.3 0.7 %copy-start.8 = (s32[8]{0:T(128)S(1)}, s32[8]{0:T(128)}, u32[]{:S(2)}) copy-start(s32[8]{0:T(128)} %len_ref.1) | copy-start | bytes 100
  14.9 0.7 %copy-start.9 = (s32[4]{0:T(128)S(1)}, s32[4]{0:T(128)}, u32[]{:S(2)}) copy-start(s32[4]{0:T(128)} %clen_ref.1) | copy-start | bytes 52

commit v2 on v1

--- a/solution.py
+++ b/solution.py
@@ -27,10 +27,11 @@
 
 def kernel(
     ns, nt, width, spans,
-    len_ref, clen_ref, q_ref, k_ref, v_ref, qd_ref, ck_ref, cv_ref, stream_ref, gain_ref, tbl_ref, w_ref,
+    len_in, clen_in, q_in, k_in, v_in, qd_in, ck_in, cv_in, stream_in, w_in, gain_ref, tbl_ref,
     att_ref, hid_ref, win_ref,
+    len_ref, clen_ref, q_ref, k_ref, v_ref, qd_ref, ck_ref, cv_ref, stream_ref,
     kbuf, vbuf, bias, mrow, lrow, acc, qdpad, qsel, qx, pout, pstat, pox, psx, wbuf, part, partx, tblx, stat, statx,
-    ks, kr, vs, vr, qs, qr, pos, por, pss, psr, ts, tr, gs, gr, ss, sr, wsem,
+    ks, kr, vs, vr, qs, qr, pos, por, pss, psr, ts, tr, gs, gr, ss, sr, loads,
 ):
     me = lax.axis_index("seq")
     mt = lax.axis_index("tp")
@@ -77,13 +78,28 @@
             for d in range(1, count)
         ]
 
-    weight_copy = pltpu.make_async_copy(w_ref, wbuf, wsem)
-    weight_copy.start()
+    places = (
+        (k_in, k_ref), (len_in, len_ref), (q_in, q_ref), (v_in, v_ref), (clen_in, clen_ref),
+        (qd_in, qd_ref), (ck_in, ck_ref), (cv_in, cv_ref), (stream_in, stream_ref), (w_in, wbuf),
+    )
+    fetches = [pltpu.make_async_copy(src, dst, loads.at[i]) for i, (src, dst) in enumerate(places)]
+    for fetch in fetches:
+        fetch.start()
     barrier = pltpu.get_barrier_semaphore()
     for d in range(1, ns):
         pl.semaphore_signal(barrier, inc=1, device_id={"seq": lax.rem(me + d, ns)}, device_id_type=MESH)
     for d in range(1, nt):
         pl.semaphore_signal(barrier, inc=1, device_id={"tp": lax.rem(mt + d, nt)}, device_id_type=MESH)
+
+    fetches[0].wait()
+    if ns + nt > 2:
+        pl.semaphore_wait(barrier, ns + nt - 2)
+    if reach:
+        @pl.when(sends(1))
+        def _():
+            relay(1, True).start()
+    for fetch in fetches[1:4]:
+        fetch.wait()
 
     ends, total = [], jnp.int32(0)
     for p in range(pairs):
@@ -98,13 +114,6 @@
     chosen = (lax.broadcasted_iota(jnp.int32, (ROW, tokens), 1) == last).astype(F32).astype(BF)
     picked = dot(chosen, q_ref[...], ((1,), (0,)))
     qsel[...] = picked.astype(BF)
-
-    if ns + nt > 2:
-        pl.semaphore_wait(barrier, ns + nt - 2)
-    if reach:
-        @pl.when(sends(1))
-        def _():
-            relay(1, True).start()
 
     q_moves = exchange(qsel, qx, qs, qr, "seq", me, ns)
     for move in q_moves:
@@ -174,6 +183,8 @@
 
     attend(0, 0)
 
+    for fetch in fetches[4:8]:
+        fetch.wait()
     for move in q_moves:
         move.wait_recv()
     q_pair = qsel[...].astype(F32)
@@ -256,7 +267,7 @@
         for kind in range(2)
     ]
     verdict_in = jnp.concatenate(sides, axis=0).astype(BF)
-    weight_copy.wait()
+    fetches[9].wait()
     part[...] = dot(verdict_in, wbuf[...], ((1,), (0,))).astype(BF)
     a_moves = exchange(part, partx, ts, tr, "tp", mt, nt)
     for move in a_moves:
@@ -269,6 +280,7 @@
 
     for move in t_moves + a_moves:
         move.wait_recv()
+    fetches[8].wait()
     rows = stream_ref.shape[0]
     table = tblx[0].astype(F32)
     added = partx[0].astype(F32)
@@ -313,6 +325,35 @@
         move.wait_send()
 
 
+def lookup(ids_in, table_in, out_ref, ids_ref, stage, lines, ids_sem, sems):
+    vocab_rows = table_in.shape[0]
+    fetch = pltpu.make_async_copy(ids_in, ids_ref, ids_sem)
+    fetch.start()
+    base = lax.axis_index("tp") * vocab_rows
+    lines[...] = jnp.zeros_like(lines)
+    fetch.wait()
+    sides, rows = ids_ref.shape
+    half = out_ref.shape[0] // sides
+    moves = []
+    for c in range(sides):
+        for r in range(rows):
+            local = ids_ref[c, r] - base
+            own = (local >= 0) & (local < vocab_rows)
+            local = jnp.where(own, local, 0)
+            spot = local & (ROW - 1)
+            top = pl.multiple_of(local - spot, ROW)
+            slot = c * rows + r
+            move = pltpu.make_async_copy(table_in.at[pl.ds(top, ROW), :], stage.at[slot], sems.at[slot])
+            move.start()
+            moves.append((move, slot, c * half + r, jnp.where(own, spot, -1)))
+    line = lax.broadcasted_iota(jnp.int32, stage.shape[1:], 0)
+    for move, slot, at, spot in moves:
+        move.wait()
+        kept = jnp.where(line == spot, stage[slot].astype(F32), 0.0)
+        lines[at : at + 1, :] = jnp.sum(kept, axis=0, keepdims=True)
+    out_ref[...] = lines[...].astype(BF)
+
+
 def shards(
     ns, nt, width,
     q_prefill, k_prefill, v_prefill, pair_lengths, q_decode, cache_k, cache_v, cache_lengths,
@@ -332,17 +373,24 @@
     cols = up(2 * heads * ROW, 128)
     half = up(rows, 16)
 
-    ids = jnp.full((2, half), -1, jnp.int32).at[:, :rows].set(verdict_ids.T).reshape(-1)
-    vocab_rows = vocab_table.shape[0]
-    local_ids = ids - jnp.where(ids >= 0, lax.axis_index("tp") * vocab_rows, 0)
-    inside = (local_ids >= 0) & (local_ids < vocab_rows)
-    table = vocab_table[jnp.clip(local_ids, 0, vocab_rows - 1)]
-    table = jnp.where(inside[:, None], table, jnp.zeros_like(table))
-
     vmem = pl.BlockSpec(memory_space=pltpu.VMEM)
-    smem = pl.BlockSpec(memory_space=pltpu.SMEM)
     peers_s, peers_t = max(ns - 1, 1), max(nt - 1, 1)
     dma = pltpu.SemaphoreType.DMA
+    hbm = pl.BlockSpec(memory_space=pltpu.HBM)
+    table = pl.pallas_call(
+        lookup,
+        out_shape=jax.ShapeDtypeStruct((2 * half, columns), BF),
+        in_specs=[hbm, hbm],
+        out_specs=vmem,
+        scratch_shapes=[
+            pltpu.SMEM((2, rows), jnp.int32),
+            pltpu.VMEM((2 * rows, ROW, columns), BF),
+            pltpu.VMEM((2 * half, columns), F32),
+            dma,
+            dma((2 * rows,)),
+        ],
+        compiler_params=pltpu.CompilerParams(vmem_limit_bytes=8 * 1024 * 1024),
+    )(verdict_ids.T, vocab_table)
     attended, hidden, win = pl.pallas_call(
         functools.partial(kernel, ns, nt, width, tuple(spans)),
         out_shape=(
@@ -350,9 +398,18 @@
             jax.ShapeDtypeStruct(stream.shape, BF),
             jax.ShapeDtypeStruct((rows, 128), F32),
         ),
-        in_specs=[smem, smem] + [vmem] * 9 + [pl.BlockSpec(memory_space=pl.ANY)],
+        in_specs=[hbm] * 10 + [vmem, vmem],
         out_specs=(vmem, vmem, vmem),
         scratch_shapes=[
+            pltpu.SMEM(pair_lengths.shape, jnp.int32),
+            pltpu.SMEM(cache_lengths.shape, jnp.int32),
+            pltpu.VMEM(q_prefill.shape, BF),
+            pltpu.VMEM(k_prefill.shape, BF),
+            pltpu.VMEM(v_prefill.shape, BF),
+            pltpu.VMEM(q_decode.shape, BF),
+            pltpu.VMEM(cache_k.shape, BF),
+            pltpu.VMEM(cache_v.shape, BF),
+            pltpu.VMEM(stream.shape, BF),
             pltpu.VMEM((slots, tokens, kv_width), BF),
             pltpu.VMEM((slots, tokens, kv_width), BF),
             pltpu.VMEM((tokens, tokens), F32),
@@ -379,14 +436,14 @@
             dma((peers_t,)), dma((peers_t,)),
             dma((peers_t,)), dma((peers_t,)),
             dma((peers_s,)), dma((peers_s,)),
-            dma,
+            dma((10,)),
         ],
         compiler_params=pltpu.CompilerParams(
             collective_id=0, has_side_effects=True, vmem_limit_bytes=48 * 1024 * 1024
         ),
     )(
         pair_lengths, cache_lengths, q_prefill, k_prefill, v_prefill, q_decode, cache_k, cache_v,
-        stream, norm_gain.reshape(1, columns), table, out_weight,
+        stream, out_weight, norm_gain.reshape(1, columns), table,
     )
     return attended, hidden, win[:, 0]
 

time: 47.6 us -> 37.1 us (0.78)
  local copies, waits for them, and re-layouts: 14.9 us -> 4.07 us
  Pallas kernels: 29.4 us -> 31.9 us
  other arithmetic: 2.08 us -> 0 us
    unnamed x22 -> x24, local copies, waits for them, and re-layouts: 11.1 us -> 2.6 us
    pallas_call x0 -> x1, Pallas kernels: none -> 2.33 us  [shards(): pl.pallas_call(lookup, out_shape=jax.ShapeDtypeStruct((2 * half, columns)...]
    gather x1 -> x0, local copies, waits for them, and re-layouts: 2.28 us -> none  [shards(): table = vocab_table[jnp.clip(local_ids, 0, vocab_rows - 1)]]
    another operation x2 -> x0, other arithmetic: 1.97 us -> none
where the time goes in v2:
time: 37.1 us; the launch traced here: 36.8 us
  Pallas kernels  31.9 us (86%)
  local copies, waits for them, and re-layouts  4.07 us (11%)
  between operations  0.8 us (2%)
    pallas_call x1, Pallas kernels, shards(): pl.pallas_call(functools.partial(kernel, ns, nt, width, tuple(spans)), ou...  29.6 us
    unnamed x24, local copies, waits for them, and re-layouts  2.6 us
    pallas_call x1, Pallas kernels, shards(): pl.pallas_call(lookup, out_shape=jax.ShapeDtypeStruct((2 * half, columns)...  2.33 us
    reshape x1, local copies, waits for them, and re-layouts, shards(): norm_gain.reshape(1, columns)  0.84 us

profile of v2, /device:TPU:0, one launch (start us, length us, event | category | flops | bytes accessed | tf_op | source)
XLA Modules:
  0.0 36.8 jit_solution(9329328734012455412)
XLA Ops:
  0.6 0.0 copy-start
  0.6 0.0 copy-start.6
  0.7 0.0 copy-start.5
  0.7 0.0 copy-start.4
  0.7 0.0 copy-start.7
  0.7 0.0 copy-start.3
  0.7 0.0 copy-start.2
  0.7 0.8 %reshape.9.gain_ref = bf16[1,2048]{1,0:T(2,128)(2,1)S(1)} reshape(bf16[2048]{0:T(1024)(128)(2,1)} %param.23) | data formatting | bytes 8192 | tf_op jit(solution)/shard_map/reshape | solution.py:446
  1.6 1.1 %copy-done.8 = s32[12,2]{0,1:T(2,128)S(1)} copy-done((s32[12,2]{0,1:T(2,128)S(1)}, s32[12,2]{0,1:T(2,128)}, u32[]{:S(2)}) %copy-start.8) | copy-done | bytes 120
  2.7 2.3 %shard_map.148.tbl_ref = bf16[32,2048]{1,0:T(8,128)(2,1)S(1)} custom-call(s32[2,12]{1,0:T(2,128)S(1)} %bitcast.1, bf16[16032,2048]{1,0:T(8,128)(2,1)} %table_in.1), custom_call_target="tpu_custom_call" | custom-call | tf_op jit(solution)/shard_map/pallas_call | solution.py:380
  5.0 0.0 copy-done
  5.0 0.0 copy-done.6
  5.1 0.0 copy-done.5
  5.1 0.0 copy-done.4
  5.1 0.0 copy-done.7
  5.1 0.0 copy-done.3
  5.1 0.0 copy-done.2
  5.1 0.0 copy-done.1
  5.1 0.0 copy-done.9
  5.1 0.0 copy-done.10
  5.1 29.6 %shard_map.149 = (bf16[256,1024]{1,0:T(8,128)(2,1)S(1)}, bf16[12,2048]{1,0:T(8,128)(2,1)S(1)}, f32[12,128]{1,0:T(8,128)S(1)}) custom-call(s32[8]{0:T(128)S(1)} %copy-done.9, s32[4]{0:T(128)S(1)} %copy-done.10, bf16[256,1024]{1,0:T(8,128)(2,1)S(1)} %copy-done.1, bf16[256,256]{1,0:T(8,128)(2,1)S(1)} %copy-done.2, bf16[256,256]{1,0:T(8,128)(2,1)S(1)} %copy-done.3, ...), custom_call_target="tpu_custom_call" | custom-call | tf_op jit(solution)/shard_map/pallas_call | solution.py:394
  34.7 0.6 %slice_reduce_fusion = f32[12]{0:T(128)} fusion(f32[12,128]{1,0:T(8,128)S(1)} %get-tuple-element.8), kind=kLoop, calls=%fused_computation | loop fusion | bytes 96 | tf_op jit(solution)/shard_map/slice | solution.py:448
  35.4 0.8 %copy.18 = bf16[256,1024]{1,0:T(8,128)(2,1)} copy(bf16[256,1024]{1,0:T(8,128)(2,1)S(1)} %get-tuple-element.12) | data formatting | bytes 1048576
  36.2 0.6 %copy.19 = bf16[12,2048]{1,0:T(8,128)(2,1)} copy(bf16[12,2048]{1,0:T(8,128)(2,1)S(1)} %get-tuple-element.13) | data formatting | bytes 98304
  (4 shorter events, 0.0 us)
Async XLA Ops:
  0.6 4.4 %copy-start = (bf16[1024,2048]{1,0:T(8,128)(2,1)S(1)}, bf16[1024,2048]{1,0:T(8,128)(2,1)}, u32[]{:S(2)}) copy-start(bf16[1024,2048]{1,0:T(8,128)(2,1)} %w_in.1) | copy-start | bytes 12582916
  0.6 4.4 %copy-start.6 = (bf16[12,2048]{1,0:T(8,128)(2,1)S(1)}, bf16[12,2048]{1,0:T(8,128)(2,1)}, u32[]{:S(2)}) copy-start(bf16[12,2048]{1,0:T(8,128)(2,1)} %stream_in.1) | copy-start | bytes 147460
  0.7 4.4 %copy-start.5 = (bf16[4,64,256]{2,1,0:T(8,128)(2,1)S(1)}, bf16[4,64,256]{2,1,0:T(8,128)(2,1)}, u32[]{:S(2)}) copy-start(bf16[4,64,256]{2,1,0:T(8,128)(2,1)} %cv_in.1) | copy-start | bytes 393220
  0.7 4.4 %copy-start.4 = (bf16[4,64,256]{2,1,0:T(8,128)(2,1)S(1)}, bf16[4,64,256]{2,1,0:T(8,128)(2,1)}, u32[]{:S(2)}) copy-start(bf16[4,64,256]{2,1,0:T(8,128)(2,1)} %ck_in.1) | copy-start | bytes 393220
  0.7 4.4 %copy-start.7 = (bf16[4,1024]{1,0:T(4,128)(2,1)S(1)}, bf16[4,1024]{1,0:T(4,128)(2,1)}, u32[]{:S(2)}) copy-start(bf16[4,1024]{1,0:T(4,128)(2,1)} %qd_in.1) | copy-start | bytes 24580
  0.7 4.4 %copy-start.3 = (bf16[256,256]{1,0:T(8,128)(2,1)S(1)}, bf16[256,256]{1,0:T(8,128)(2,1)}, u32[]{:S(2)}) copy-start(bf16[256,256]{1,0:T(8,128)(2,1)} %v_in.1) | copy-start | bytes 393220
  0.7 4.4 %copy-start.2 = (bf16[256,256]{1,0:T(8,128)(2,1)S(1)}, bf16[256,256]{1,0:T(8,128)(2,1)}, u32[]{:S(2)}) copy-start(bf16[256,256]{1,0:T(8,128)(2,1)} %k_in.1) | copy-start | bytes 393220
  0.7 4.4 %copy-start.1 = (bf16[256,1024]{1,0:T(8,128)(2,1)S(1)}, bf16[256,1024]{1,0:T(8,128)(2,1)}, u32[]{:S(2)}) copy-start(bf16[256,1024]{1,0:T(8,128)(2,1)} %q_in.1) | copy-start | bytes 1572868
  1.6 1.1 %copy-start.8 = (s32[12,2]{0,1:T(2,128)S(1)}, s32[12,2]{0,1:T(2,128)}, u32[]{:S(2)}) copy-start(s32[12,2]{0,1:T(2,128)} %param.25) | copy-start | bytes 292
  2.7 2.4 %copy-start.9 = (s32[8]{0:T(128)S(1)}, s32[8]{0:T(128)}, u32[]{:S(2)}) copy-start(s32[8]{0:T(128)} %len_in.1) | copy-start | bytes 100
  2.7 2.4 %copy-start.10 = (s32[4]{0:T(128)S(1)}, s32[4]{0:T(128)}, u32[]{:S(2)}) copy-start(s32[4]{0:T(128)} %clen_in.1) | copy-start | bytes 52
